TPU v7x, 32 devices: a whole 2x2x4 slice. The times are simulated.
32 devices in a mesh: grp: 2 (over x), exp: 16 (over z, y, core).
Axes of the slice: x: 2, y: 2, z: 4, core: 2. Of those that a mesh axis runs over, the one named last changes fastest.
Arguments:
- tokens: bfloat16 [192, 196, 768], P(('grp', 'exp')), parts along dimension 0, may hold values from -6 to 6
- logits: float32 [192, 196, 16], P(('grp', 'exp')), parts along dimension 0, may hold values from -8 to 400
- slot_out: bfloat16 [32, 96, 768], P(('grp', 'exp')), parts along dimension 0, may hold values from -1.5 to 1.5
- slot_in: bfloat16 [32, 96, 768], P(('grp', 'exp')), parts along dimension 0, may hold values from -6 to 6
- out_grad: bfloat16 [192, 196, 768], P(('grp', 'exp')), parts along dimension 0, may hold values from -192 to 192
- router: bfloat16 [16, 768], replicated, may hold values from -0.21875 to 0.21875
- w_in: bfloat16 [16, 768, 3072], P('exp'), may hold values from -0.21875 to 0.21875
- bias_in: float32 [16, 3072], P('exp'), may hold values from -5 to 5
- w_out: bfloat16 [16, 3072, 768], P('exp'), may hold values from -0.109375 to 0.109375
Outputs:
- input_grad: bfloat16 [192, 196, 768], P(('grp', 'exp')), parts along dimension 0
- router_grad: float32 [32, 768], P(('grp', 'exp')), parts along dimension 0
There are 2 independent parts, one for each index of `grp`. A program takes and returns all parts, laid end to end along the dimension named above; an argument that names none is the same for every part. Nothing has to cross between parts.
All inputs are finite; a program needn't handle non-finite values.
Results may differ from a plain program's by a relative error of at most 0.0075.
Values may be sent and summed in bfloat16 or wider, within the bound.
A program may use at most 64 MiB of HBM per device.

v0:
```python
import jax
import jax.numpy as jnp
from jax import lax
from jax.sharding import PartitionSpec as P

gelu_root = 0.7978845608028654
gelu_cubic = 0.044715


def gelu_slope(values):
    inner_arg = gelu_root * (values + gelu_cubic * values * values * values)
    tanh_val = jnp.tanh(inner_arg)
    return 0.5 * (1.0 + tanh_val) + 0.5 * values * (1.0 - tanh_val * tanh_val) * gelu_root * (
        1.0 + 3.0 * gelu_cubic * values * values
    )


def router_term(grads, tokens):

    def term(offset, amount):
        return jnp.einsum("itj,itd->jd", grads, tokens, preferred_element_type=jnp.float32)

    return term


def on_device(tokens, logits, slot_out, slot_in, out_grad, router, w_in, bias_in, w_out):
    images = tokens.shape[0]
    width = tokens.shape[2]
    peers = lax.axis_size("exp")
    dispatch = jax.nn.softmax(logits, axis=1)
    combine = jax.nn.softmax(logits, axis=2)
    combine_rounded = combine.astype(jnp.bfloat16)
    dispatch_rounded = dispatch.astype(jnp.bfloat16)
    slot_grad = jnp.einsum(
        "itj,itd->jid", combine_rounded, out_grad, preferred_element_type=jnp.float32
    ).astype(jnp.bfloat16)
    received = lax.all_to_all(slot_grad[:, None], "exp", split_axis=0, concat_axis=1, tiled=True)
    held_outputs = slot_out.reshape(1, peers, images, width)
    fetched = lax.all_to_all(held_outputs, "exp", split_axis=1, concat_axis=0, tiled=True)
    hidden_pre = jnp.dot(slot_in[0], w_in[0], preferred_element_type=jnp.float32) + bias_in[0]
    hidden_grad = jnp.einsum(
        "rd,fd->rf",
        received.reshape(peers * images, width),
        w_out[0],
        preferred_element_type=jnp.float32,
    )
    pre_grad = (hidden_grad * gelu_slope(hidden_pre)).astype(jnp.bfloat16)
    returned = jnp.einsum(
        "rf,df->rd", pre_grad, w_in[0], preferred_element_type=jnp.float32
    ).astype(jnp.bfloat16)
    returned = returned.reshape(1, peers, images, width)
    back = lax.all_to_all(returned, "exp", split_axis=1, concat_axis=0, tiled=True)
    slot_in_grad = back.reshape(peers, images, width)
    slot_outputs = fetched.reshape(peers, images, width)
    combine_grad = jnp.einsum(
        "itd,jid->itj", out_grad, slot_outputs, preferred_element_type=jnp.float32
    )
    comb_logit = (
        combine * (combine_grad - jnp.sum(combine * combine_grad, axis=2, keepdims=True))
    ).astype(jnp.bfloat16)
    total_images = images * peers
    rows_kept = router.shape[0] // peers
    dispatch_grad = jnp.einsum(
        "itd,jid->itj", tokens, slot_in_grad, preferred_element_type=jnp.float32
    )
    disp_logit = (
        dispatch * (dispatch_grad - jnp.sum(dispatch * dispatch_grad, axis=1, keepdims=True))
    ).astype(jnp.bfloat16)
    comb_fn = router_term(comb_logit, tokens)
    disp_fn = router_term(disp_logit, tokens)
    offset = jnp.int32(0)
    router_grad = (
        lax.psum_scatter(
            comb_fn(offset, rows_kept * lax.axis_size("exp"))
            + disp_fn(offset, rows_kept * lax.axis_size("exp")),
            "exp",
            scatter_dimension=0,
            tiled=True,
        )
        / total_images
    )
    input_grad = jnp.einsum(
        "itj,jid->itd", dispatch_rounded, slot_in_grad, preferred_element_type=jnp.float32
    )
    input_grad = input_grad + jnp.einsum(
        "itj,jd->itd", comb_logit, router, preferred_element_type=jnp.float32
    )
    input_grad = input_grad + jnp.einsum(
        "itj,jd->itd", disp_logit, router, preferred_element_type=jnp.float32
    )
    return (input_grad.astype(jnp.bfloat16), router_grad)


def solution(mesh):
    placed = (
        P(("grp", "exp"), None, None),
        P(("grp", "exp"), None, None),
        P(("grp", "exp"), None, None),
        P(("grp", "exp"), None, None),
        P(("grp", "exp"), None, None),
        P(),
        P("exp", None, None),
        P("exp", None),
        P("exp", None, None),
    )
    return jax.shard_map(
        on_device,
        mesh=mesh,
        in_specs=placed,
        out_specs=(P(("grp", "exp"), None, None), P(("grp", "exp"), None)),
        check_vma=False,
    )
```

profile of v0, /device:TPU:0, one launch (start us, length us, event | category | flops | bytes accessed | tf_op | source)
XLA Modules:
  0.0 118.8 jit_solution(1337021124670407164)
XLA Ops:
  0.6 0.0 copy-start
  0.6 0.0 copy-start.5
  0.7 1.1 fusion.57
  1.8 0.5 copy-done
  2.2 1.3 %fusion.25 = bf16[16,1,6,768]{3,0,2,1:T(8,128)(2,1)S(1)} fusion(bf16[6,196,768]{2,1,0:T(8,128)(2,1)S(1)} %copy-done, f32[6,196]{1,0:T(8,128)S(1)} %get-tuple-element.2, f32[6,196,16]{1,2,0:T(8,128)} %param.10), kind=kOutput, calls=%fused_computation.21 | convolution fusion | flops 29032744 | bytes 2033760 | tf_op jit(solution)/shard_map/itj,itd->jid/dot_general | solution.py:34
  3.6 0.7 copy.15
  4.3 7.4 %all-to-all-start = ((bf16[16,1,6,768]{3,2,1,0:T(8,128)(2,1)}), bf16[16,1,6,768]{3,2,1,0:T(8,128)(2,1)S(1)}, u32[]{:S(2)}, u32[]{:S(2)}) async-start(bf16[16,1,6,768]{3,2,1,0:T(8,128)(2,1)} %copy.15), calls=%async_computation | async-start | bytes 393216 | tf_op jit(solution)/shard_map/all_to_all | solution.py:37
  11.7 0.0 copy-done.5
  11.7 0.0 copy-start.6
  11.8 0.0 copy-start.3
  11.8 3.3 %fusion.11 = f32[96,3072]{1,0:T(8,128)S(1)} fusion(bf16[1,768,3072]{2,1,0:T(8,128)(2,1)} %param.15, f32[3072]{0:T(1024)S(1)} %bitcast.69, bf16[1,96,768]{2,1,0:T(8,128)(2,1)} %param.12), kind=kOutput, calls=%fused_computation.10 | convolution fusion | flops 453279744 | bytes 6057984 | tf_op jit(solution)/shard_map/dot_general | solution.py:40
  15.1 1.6 %reshape.40 = bf16[1,16,6,768]{3,2,1,0:T(8,128)(2,1)} reshape(bf16[1,96,768]{2,1,0:T(8,128)(2,1)} %param.11) | data formatting | bytes 294912 | tf_op jit(solution)/shard_map/reshape | solution.py:38
  16.8 0.0 copy-done.6
  16.8 0.7 dynamic-slice
  17.4 0.0 copy-done.3
  17.4 1.0 fusion.58
  18.4 2.3 %all-to-all-done = bf16[16,1,6,768]{3,2,1,0:T(8,128)(2,1)S(1)} async-done(((bf16[16,1,6,768]{3,2,1,0:T(8,128)(2,1)}), bf16[16,1,6,768]{3,2,1,0:T(8,128)(2,1)S(1)}, u32[]{:S(2)}, u32[]{:S(2)}) %all-to-all-start) | async-done | bytes 147488 | tf_op jit(solution)/shard_map/all_to_all | solution.py:37
  20.7 4.2 %all-to-all-start.2 = ((bf16[1,16,6,768]{3,2,0,1:T(8,128)(2,1)}), bf16[1,16,6,768]{3,2,0,1:T(8,128)(2,1)}, u32[]{:S(2)}, u32[]{:S(2)}) async-start(bf16[1,16,6,768]{3,2,0,1:T(8,128)(2,1)} %bitcast.68), calls=%async_computation.2 | async-start | bytes 393216 | tf_op jit(solution)/shard_map/all_to_all | solution.py:39
  24.9 0.7 reshape.37
  25.6 6.9 %fusion.22 = bf16[96,768]{1,0:T(8,128)(2,1)S(1)} fusion(bf16[1,768,3072]{2,1,0:T(8,128)(2,1)} %param.15, bf16[96,768]{1,0:T(8,128)(2,1)} %reshape.37, bf16[1,3072,768]{2,1,0:T(8,128)(2,1)} %param.17, f32[96,3072]{1,0:T(8,128)S(1)} %fusion.11), kind=kOutput, calls=%fused_computation.19 | convolution fusion | flops 911646720 | bytes 10911744 | tf_op jit(solution)/shard_map/rf,df->rd/dot_general | solution.py:48
  32.5 0.7 reshape.38
  33.2 0.7 all-to-all-done.2
  33.9 5.3 %all-to-all-start.1 = ((bf16[1,16,6,768]{3,2,0,1:T(8,128)(2,1)}), bf16[1,16,6,768]{3,2,0,1:T(8,128)(2,1)S(1)}, u32[]{:S(2)}, u32[]{:S(2)}) async-start(bf16[1,16,6,768]{3,2,0,1:T(8,128)(2,1)} %bitcast.6), calls=%async_computation.1 | async-start | bytes 393216 | tf_op jit(solution)/shard_map/all_to_all | solution.py:52
  39.1 0.0 copy-start.1
  39.1 0.0 copy-start.4
  39.1 1.7 %multiply_reduce_fusion.1 = (f32[6,196]{1,0:T(8,128)S(1)}, f32[6,196,16]{1,2,0:T(8,128)S(1)}) fusion(f32[6,196,16]{1,2,0:T(8,128)S(1)} %get-tuple-element.3, f32[6,196]{1,0:T(8,128)S(1)} %get-tuple-element.2, bf16[6,196,768]{2,1,0:T(8,128)(2,1)S(1)} %copy-done, bf16[1,16,6,768]{3,2,0,1:T(8,128)(2,1)} %all-to-all-done.2), kind=kOutput, calls=%fused_computation.47 | convolution fusion | flops 28956648 | bytes 2113728 | tf_op jit(solution)/shard_map/itd,jid->itj/dot_general | solution.py:55
  40.8 0.0 copy-done.1
  40.8 0.4 convolution_bitcast_fusion.2
  41.2 0.0 copy-done.4
  41.2 2.5 %fusion.50 = f32[6,196,768]{2,1,0:T(8,128)} fusion(bf16[6,196,16]{1,2,0:T(8,128)(2,1)S(1)} %multiply_convert_fusion.1, bf16[16,768]{1,0:T(8,128)(2,1)S(1)} %copy-done.4), kind=kOutput, calls=%fused_computation.53 | convolution fusion | flops 28901376 | bytes 3674880 | tf_op jit(solution)/shard_map/itj,jd->itd/dot_general | solution.py:85
  43.7 4.3 %all-to-all-done.1 = bf16[1,16,6,768]{3,2,0,1:T(8,128)(2,1)S(1)} async-done(((bf16[1,16,6,768]{3,2,0,1:T(8,128)(2,1)}), bf16[1,16,6,768]{3,2,0,1:T(8,128)(2,1)S(1)}, u32[]{:S(2)}, u32[]{:S(2)}) %all-to-all-start.1) | async-done | bytes 147488 | tf_op jit(solution)/shard_map/all_to_all | solution.py:52
  48.1 0.0 copy-start.2
  48.1 2.3 %multiply_reduce_fusion = (f32[6,16]{1,0:T(8,128)S(1)}, f32[6,196,16]{1,2,0:T(8,128)S(1)}) fusion(f32[6,196,16]{1,2,0:T(8,128)S(1)} %get-tuple-element.5, f32[6,16]{1,0:T(8,128)S(1)} %get-tuple-element.4, bf16[6,196,768]{2,1,0:T(8,128)(2,1)} %param.9, bf16[1,16,6,768]{3,2,0,1:T(8,128)(2,1)S(1)} %all-to-all-done.1), kind=kOutput, calls=%fused_computation.45 | convolution fusion | flops 28957728 | bytes 2105088 | tf_op jit(solution)/shard_map/itd,jid->itj/dot_general | solution.py:63
  50.4 0.1 multiply_convert_fusion
  50.5 0.0 copy-done.2
  50.5 0.4 fusion.30
  50.9 58.6 %all-reduce = f32[16,768]{1,0:T(8,128)S(1)} all-reduce(f32[16,768]{1,0:T(8,128)S(1)} %fusion.30), channel_id=2, replica_groups=mesh['grp'=2,'exp'=16] {'exp'}, use_global_device_ids=true, to_apply=%region_6.0.clone | all-reduce | flops 12288 | bytes 98304
  109.5 1.3 %dynamic-slice_multiply_fusion = f32[1,768]{1,0:T(1,128)} fusion(f32[16,768]{1,0:T(8,128)S(1)} %all-reduce, u32[]{:T(128)} %bitcast.15), kind=kLoop, calls=%fused_computation.55 | loop fusion | flops 768 | bytes 6148 | tf_op jit(solution)/shard_map/div | solution.py:73
  110.8 2.9 %fusion.41 = f32[6,196,768]{2,1,0:T(8,128)} fusion(bf16[1,16,6,768]{3,2,0,1:T(8,128)(2,1)S(1)} %all-to-all-done.1, f32[6,16]{1,0:T(8,128)S(1)} %get-tuple-element.4, f32[6,196,16]{1,2,0:T(8,128)S(1)} %copy-done.3), kind=kOutput, calls=%fused_computation.38 | convolution fusion | flops 28958116 | bytes 3835776 | tf_op jit(solution)/shard_map/itj,jid->itd/dot_general | solution.py:82
  113.7 5.1 %add_convert_fusion = bf16[6,196,768]{2,1,0:T(8,128)(2,1)} fusion(f32[6,196,768]{2,1,0:T(8,128)} %fusion.41, f32[6,196,768]{2,1,0:T(8,128)} %fusion.50, bf16[6,196,16]{1,2,0:T(8,128)(2,1)S(1)} %multiply_convert_fusion, bf16[16,768]{1,0:T(8,128)(2,1)S(1)} %copy-done.4), kind=kOutput, calls=%fused_computation.8 | convolution fusion | flops 31610880 | bytes 9093888 | tf_op jit(solution)/shard_map/itj,jd->itd/dot_general | solution.py:88
  (1 shorter events, 0.0 us)
Async XLA Ops:
  0.6 1.6 %copy-start = (bf16[6,196,768]{2,1,0:T(8,128)(2,1)S(1)}, bf16[6,196,768]{2,1,0:T(8,128)(2,1)}, u32[]{:S(2)}) copy-start(bf16[6,196,768]{2,1,0:T(8,128)(2,1)} %param.13) | copy-start | bytes 5419012
  0.6 11.1 %copy-start.5 = (f32[1,3072]{1,0:T(1,128)S(1)}, f32[1,3072]{1,0:T(1,128)}, u32[]{:S(2)}) copy-start(f32[1,3072]{1,0:T(1,128)} %param.16) | copy-start | bytes 36868
  4.3 16.4 %all-to-all-start = ((bf16[16,1,6,768]{3,2,1,0:T(8,128)(2,1)}), bf16[16,1,6,768]{3,2,1,0:T(8,128)(2,1)S(1)}, u32[]{:S(2)}, u32[]{:S(2)}) async-start(bf16[16,1,6,768]{3,2,1,0:T(8,128)(2,1)} %copy.15), calls=%async_computation | async-start | bytes 393216 | tf_op jit(solution)/shard_map/all_to_all | solution.py:37
  11.7 5.0 %copy-start.6 = (u32[32]{0:T(128)S(1)}, u32[32]{0:T(128)}, u32[]{:S(2)}) copy-start(u32[32]{0:T(128)} %constant.29) | copy-start | bytes 388
  11.8 5.7 %copy-start.3 = (f32[6,196,16]{1,2,0:T(8,128)S(1)}, f32[6,196,16]{1,2,0:T(8,128)}, u32[]{:S(2)}) copy-start(f32[6,196,16]{1,2,0:T(8,128)} %param.10) | copy-start | bytes 225796
  20.7 13.2 %all-to-all-start.2 = ((bf16[1,16,6,768]{3,2,0,1:T(8,128)(2,1)}), bf16[1,16,6,768]{3,2,0,1:T(8,128)(2,1)}, u32[]{:S(2)}, u32[]{:S(2)}) async-start(bf16[1,16,6,768]{3,2,0,1:T(8,128)(2,1)} %bitcast.68), calls=%async_computation.2 | async-start | bytes 393216 | tf_op jit(solution)/shard_map/all_to_all | solution.py:39
  33.9 14.2 %all-to-all-start.1 = ((bf16[1,16,6,768]{3,2,0,1:T(8,128)(2,1)}), bf16[1,16,6,768]{3,2,0,1:T(8,128)(2,1)S(1)}, u32[]{:S(2)}, u32[]{:S(2)}) async-start(bf16[1,16,6,768]{3,2,0,1:T(8,128)(2,1)} %bitcast.6), calls=%async_computation.1 | async-start | bytes 393216 | tf_op jit(solution)/shard_map/all_to_all | solution.py:52
  39.1 1.7 %copy-start.1 = (bf16[6,196,768]{2,1,0:T(8,128)(2,1)S(1)}, bf16[6,196,768]{2,1,0:T(8,128)(2,1)}, u32[]{:S(2)}) copy-start(bf16[6,196,768]{2,1,0:T(8,128)(2,1)} %param.9) | copy-start | bytes 5419012
  39.1 2.1 %copy-start.4 = (bf16[16,768]{1,0:T(8,128)(2,1)S(1)}, bf16[16,768]{1,0:T(8,128)(2,1)}, u32[]{:S(2)}) copy-start(bf16[16,768]{1,0:T(8,128)(2,1)} %param.14) | copy-start | bytes 73732
  48.1 2.4 %copy-start.2 = (bf16[6,196,768]{2,1,0:T(8,128)(2,1)S(1)}, bf16[6,196,768]{2,1,0:T(8,128)(2,1)}, u32[]{:S(2)}) copy-start(bf16[6,196,768]{2,1,0:T(8,128)(2,1)} %param.9) | copy-start | bytes 5419012
where the time goes:
time: 119 us
  blocking collectives  58.6 us (49%)
  matrix products  26.8 us (23%)
  starting transfers between devices  16.8 us (14%)
  waiting for transfers between devices  7.3 us (6%)
  local copies, waits for them, and re-layouts  4.98 us (4%)
  other arithmetic  3.51 us (3%)
    unnamed x1, blocking collectives  58.6 us
    all_to_all x1, starting transfers between devices, on_device(): lax.all_to_all(slot_grad[:, None], 'exp', split_axis=0, concat_axis=1, ti...  7.41 us
    dot_general x1, matrix products, on_device(): jnp.einsum('rf,df->rd', pre_grad, w_in[0], preferred_element_type=jnp.flo...  6.86 us
    all_to_all x1, starting transfers between devices, on_device(): lax.all_to_all(returned, 'exp', split_axis=1, concat_axis=0, tiled=True)  5.25 us
    dot_general x1, matrix products, on_device(): jnp.einsum('itj,jd->itd', disp_logit, router, preferred_element_type=jnp....  5.08 us
    all_to_all x1, waiting for transfers between devices, on_device(): lax.all_to_all(returned, 'exp', split_axis=1, concat_axis=0, tiled=True)  4.34 us
    all_to_all x1, starting transfers between devices, on_device(): lax.all_to_all(held_outputs, 'exp', split_axis=1, concat_axis=0, tiled=True)  4.17 us
    dot_general x1, matrix products, on_device(): jnp.dot(slot_in[0], w_in[0], preferred_element_type=jnp.float32)  3.34 us
  transfers between devices with their start and end apart: 3, of which 3 were waited for; matrix products, arithmetic and copies ran while one was open for 16% of the time, Pallas kernels for 0%

commit v1 on v0

v1 whole, which is shorter than its diff:
```python
import functools

import jax
import jax.numpy as jnp
from jax import lax
from jax.experimental import pallas as pl
from jax.experimental.pallas import tpu as pltpu
from jax.sharding import PartitionSpec as P

gelu_root = 0.7978845608028654
gelu_cubic = 0.044715
MESH = pl.DeviceIdType.MESH
F32 = jnp.float32
BF16 = jnp.bfloat16


def gelu_slope(values):
    square = values * values
    inner_arg = gelu_root * (values + gelu_cubic * square * values)
    tanh_val = jnp.tanh(inner_arg)
    return 0.5 * (1.0 + tanh_val) + 0.5 * values * (1.0 - tanh_val * tanh_val) * gelu_root * (
        1.0 + 3.0 * gelu_cubic * square
    )


def dot(a, b):
    return lax.dot_general(a, b, (((1,), (0,)), ((), ())), preferred_element_type=F32)


def dot_nt(a, b):
    return lax.dot_general(a, b, (((1,), (1,)), ((), ())), preferred_element_type=F32)


def dot_tn(a, b):
    return lax.dot_general(a, b, (((0,), (0,)), ((), ())), preferred_element_type=F32)


def ones_where(rows, cols, wanted):
    r = lax.broadcasted_iota(jnp.int32, (rows, cols), 0)
    c = lax.broadcasted_iota(jnp.int32, (rows, cols), 1)
    return jnp.where(wanted(r, c), 1.0, 0.0).astype(BF16)


def body(
    n, b, pad, chunk,
    tok_hbm, log_hbm, so_hbm, si_hbm, og_hbm, rt_hbm, wi_hbm, bi_hbm, wo_hbm,
    ig_hbm, rg_ref,
    tok, logv, so, si, og, rt, wi, bi, wo, igv,
    comb, disp, combl, displ, slope, sg, sip,
    send_s, recv_s, send_a, recv_a, send_b, recv_b, send_r, recv_r,
    load_sem, out_sem, ss, rs, sa, ra, sb, rb, sr, rr,
):
    me = lax.axis_index("exp")
    width = tok.shape[2]
    hidden = wi.shape[2]
    rows = n * b
    padded = n * pad

    loads = {}
    pairs = [
        ("log", log_hbm, logv), ("og", og_hbm, og), ("so", so_hbm, so), ("si", si_hbm, si),
        ("wi", wi_hbm, wi), ("bi", bi_hbm, bi), ("wo", wo_hbm, wo), ("tok", tok_hbm, tok), ("rt", rt_hbm, rt),
    ]
    for at, (name, src, dst) in enumerate(pairs):
        loads[name] = pltpu.make_async_copy(src, dst, load_sem.at[at])
        loads[name].start()

    barrier = pltpu.get_barrier_semaphore()

    def greet(d, _):
        peer = lax.rem(me + d, n)
        pl.semaphore_signal(barrier, inc=1, device_id={"exp": peer}, device_id_type=MESH)
        return 0

    lax.fori_loop(1, n, greet, 0)

    def remote(src, dst, send_sem, recv_sem, peer, slot):
        return pltpu.make_async_remote_copy(
            src_ref=src.at[peer], dst_ref=dst.at[slot], send_sem=send_sem.at[peer],
            recv_sem=recv_sem.at[slot], device_id={"exp": peer}, device_id_type=MESH,
        )

    def send_all(src, dst, send_sem, recv_sem):
        def step(d, _):
            remote(src, dst, send_sem, recv_sem, lax.rem(me + d, n), me).start()
            return 0

        lax.fori_loop(1, n, step, 0)
        dst[me] = src[me]

    def wait_all(src, dst, send_sem, recv_sem):
        def step(d, _):
            peer = lax.rem(me + n - d, n)
            remote(src, dst, send_sem, recv_sem, peer, peer).wait_recv()
            return 0

        lax.fori_loop(1, n, step, 0)

    def drain(src, dst, send_sem, recv_sem):
        def step(d, _):
            remote(src, dst, send_sem, recv_sem, lax.rem(me + d, n), me).wait_send()
            return 0

        lax.fori_loop(1, n, step, 0)

    spread = ones_where(padded, rows, lambda r, c: (r % pad < b) & (c == (r // pad) * b + r % pad))
    to_peers = ones_where(padded, rows, lambda r, c: (r % pad < b) & (c == (r % pad) * n + r // pad))
    to_images = ones_where(rows, padded, lambda r, c: c == (r % n) * pad + r // n)

    def grouped(x):
        return x.reshape(n, pad, width).astype(BF16)

    def flat(x):
        return x.astype(F32).reshape(padded, width).astype(BF16)

    loads["so"].wait()
    send_s[...] = grouped(dot(spread, so[0]))
    pl.semaphore_wait(barrier, n - 1)
    send_all(send_s, recv_s, ss, rs)

    loads["log"].wait()
    loads["og"].wait()
    for i in range(b):
        lt = logv[i].T
        e = jnp.exp(lt - jnp.max(lt, axis=0, keepdims=True))
        c = e / jnp.sum(e, axis=0, keepdims=True)
        comb[i] = c
        sg[i * n:(i + 1) * n, :] = dot(c.astype(BF16), og[i]).astype(BF16)
    send_a[...] = grouped(dot(to_peers, sg[...]))
    send_all(send_a, recv_a, sa, ra)

    for i in range(b):
        lt = logv[i].T
        e = jnp.exp(lt - jnp.max(lt, axis=1, keepdims=True))
        disp[i] = e / jnp.sum(e, axis=1, keepdims=True)

    loads["si"].wait()
    sip[...] = dot(spread, si[0]).astype(BF16)
    loads["wi"].wait()
    loads["bi"].wait()
    for k in range(0, hidden, chunk):
        hp = dot(sip[...], wi[0, :, k:k + chunk]) + bi[:, k:k + chunk]
        slope[:, k:k + chunk] = gelu_slope(hp)

    loads["wo"].wait()
    wait_all(send_a, recv_a, sa, ra)
    got = flat(recv_a[...])
    acc = jnp.zeros((padded, width), F32)
    for k in range(0, hidden, chunk):
        hg = dot_nt(got, wo[0, k:k + chunk, :])
        pre = (hg * slope[:, k:k + chunk]).astype(BF16)
        acc = acc + dot_nt(pre, wi[0, :, k:k + chunk])
    send_b[...] = grouped(acc)
    send_all(send_b, recv_b, sb, rb)

    loads["tok"].wait()
    loads["rt"].wait()
    wait_all(send_s, recv_s, ss, rs)
    outs = dot(to_images, flat(recv_s[...])).astype(BF16)
    racc = jnp.zeros((n, width), F32)
    for i in range(b):
        cg = dot_nt(outs[i * n:(i + 1) * n, :], og[i])
        c = comb[i]
        cl = (c * (cg - jnp.sum(c * cg, axis=0, keepdims=True))).astype(BF16)
        combl[i] = cl
        racc = racc + dot(cl, tok[i])

    wait_all(send_b, recv_b, sb, rb)
    sg[...] = dot(to_images, flat(recv_b[...])).astype(BF16)
    for i in range(b):
        dg = dot_nt(sg[i * n:(i + 1) * n, :], tok[i])
        d = disp[i]
        dl = (d * (dg - jnp.sum(d * dg, axis=1, keepdims=True))).astype(BF16)
        displ[i] = dl
        racc = racc + dot(dl, tok[i])
    send_r[...] = racc.reshape(n, 1, width)
    send_all(send_r, recv_r, sr, rr)

    outs_dma = []
    for i in range(b):
        left = jnp.concatenate([disp[i].astype(BF16), combl[i], displ[i]], axis=0)
        right = jnp.concatenate([sg[i * n:(i + 1) * n, :], rt[...], rt[...]], axis=0)
        igv[i] = dot_tn(left, right).astype(BF16)
        copy = pltpu.make_async_copy(igv.at[i], ig_hbm.at[i], out_sem.at[i])
        copy.start()
        outs_dma.append(copy)

    wait_all(send_r, recv_r, sr, rr)
    rg_ref[...] = jnp.sum(recv_r[...], axis=0) / (n * b)
    drain(send_s, recv_s, ss, rs)
    drain(send_a, recv_a, sa, ra)
    drain(send_b, recv_b, sb, rb)
    drain(send_r, recv_r, sr, rr)
    for copy in outs_dma:
        copy.wait()


def on_device(tokens, logits, slot_out, slot_in, out_grad, router, w_in, bias_in, w_out):
    b, seq, width = tokens.shape
    n = lax.axis_size("exp")
    hidden = w_in.shape[2]
    pad = -(-b // 8) * 8
    padded = n * pad
    chunk = 768 if hidden % 768 == 0 else hidden
    any_spec = pl.BlockSpec(memory_space=pl.ANY)
    exchange = pltpu.VMEM((n, pad, width), BF16)
    small = pltpu.VMEM((n, 1, width), F32)
    sems = pltpu.SemaphoreType.DMA((n,))
    return pl.pallas_call(
        functools.partial(body, n, b, pad, chunk),
        out_shape=(
            jax.ShapeDtypeStruct((b, seq, width), BF16),
            jax.ShapeDtypeStruct((1, width), F32),
        ),
        in_specs=[any_spec] * 9,
        out_specs=(any_spec, pl.BlockSpec(memory_space=pltpu.VMEM)),
        scratch_shapes=[
            pltpu.VMEM(tokens.shape, BF16),
            pltpu.VMEM(logits.shape, F32),
            pltpu.VMEM(slot_out.shape, BF16),
            pltpu.VMEM(slot_in.shape, BF16),
            pltpu.VMEM(out_grad.shape, BF16),
            pltpu.VMEM(router.shape, BF16),
            pltpu.VMEM(w_in.shape, BF16),
            pltpu.VMEM(bias_in.shape, F32),
            pltpu.VMEM(w_out.shape, BF16),
            pltpu.VMEM((b, seq, width), BF16),
            pltpu.VMEM((b, n, seq), F32),
            pltpu.VMEM((b, n, seq), F32),
            pltpu.VMEM((b, n, seq), BF16),
            pltpu.VMEM((b, n, seq), BF16),
            pltpu.VMEM((padded, hidden), F32),
            pltpu.VMEM((n * b, width), BF16),
            pltpu.VMEM((padded, width), BF16),
            exchange, exchange, exchange, exchange, exchange, exchange, small, small,
            pltpu.SemaphoreType.DMA((9,)),
            pltpu.SemaphoreType.DMA((b,)),
            sems, sems, sems, sems, sems, sems, sems, sems,
        ],
        compiler_params=pltpu.CompilerParams(
            collective_id=0, has_side_effects=True, vmem_limit_bytes=60 * 1024 * 1024
        ),
        name="moe_input_grad",
    )(tokens, logits, slot_out, slot_in, out_grad, router, w_in, bias_in, w_out)


def solution(mesh):
    placed = (
        P(("grp", "exp"), None, None),
        P(("grp", "exp"), None, None),
        P(("grp", "exp"), None, None),
        P(("grp", "exp"), None, None),
        P(("grp", "exp"), None, None),
        P(),
        P("exp", None, None),
        P("exp", None),
        P("exp", None, None),
    )
    return jax.shard_map(
        on_device,
        mesh=mesh,
        in_specs=placed,
        out_specs=(P(("grp", "exp"), None, None), P(("grp", "exp"), None)),
        check_vma=False,
    )
```

time: 119 us -> 40.8 us (0.34)
  blocking collectives: 58.6 us -> 0 us
  Pallas kernels: 0 us -> 34.6 us
  matrix products: 26.8 us -> 0 us
  starting transfers between devices: 16.8 us -> 0 us
  waiting for transfers between devices: 7.3 us -> 0 us
  other arithmetic: 3.51 us -> 0 us
    unnamed x1 -> x0, blocking collectives: 58.6 us -> none
    pallas_call x0 -> x1, Pallas kernels: none -> 34.6 us  [on_device(): pl.pallas_call(functools.partial(body, n, b, pad, chunk), out_shape=(jax....]
    dot_general x10 -> x0, matrix products: 26.8 us -> none  [the longest x1 6.86 us: on_device(): jnp.einsum('rf,df->rd', pre_grad, w_in[0], preferred_element_type=jnp.flo...]
    all_to_all x3 -> x0, starting transfers between devices: 16.8 us -> none  [the longest x1 7.41 us: on_device(): lax.all_to_all(slot_grad[:, None], 'exp', split_axis=0, concat_axis=1, ti...]
    all_to_all x3 -> x0, waiting for transfers between devices: 7.3 us -> none  [the longest x1 4.34 us: on_device(): lax.all_to_all(returned, 'exp', split_axis=1, concat_axis=0, tiled=True)]
    unnamed x15 -> x5, local copies, waits for them, and re-layouts: 1.16 us -> 5.38 us
    reshape x3 -> x0, local copies, waits for them, and re-layouts: 3.08 us -> none  [the longest x1 1.63 us: on_device(): held_outputs = slot_out.reshape(1, peers, images, width)]
    sub x2 -> x0, other arithmetic: 2.1 us -> none  [the longest x1 1.12 us: on_device(): combine = jax.nn.softmax(logits, axis=2)]
  transfers between devices with their start and end apart: 3 -> 0, of which waited for: 3 -> 0; matrix products, arithmetic and copies ran while one was open for 16% -> 0% of each run, Pallas kernels for 0% -> 0%
where the time goes in v1:
time: 40.8 us; the launch traced here: 40.6 us
  Pallas kernels  34.6 us (85%)
  local copies, waits for them, and re-layouts  5.38 us (13%)
  between operations  0.65 us (2%)
    pallas_call x1, Pallas kernels, on_device(): pl.pallas_call(functools.partial(body, n, b, pad, chunk), out_shape=(jax....  34.6 us
    unnamed x5, local copies, waits for them, and re-layouts  5.38 us

profile of v1, /device:TPU:0, one launch (start us, length us, event | category | flops | bytes accessed | tf_op | source)
XLA Modules:
  0.0 40.6 jit_solution(4780457362658312733)
XLA Ops:
  0.6 1.9 %copy.11.log_hbm = f32[6,196,16]{2,1,0:T(8,128)} copy(f32[6,196,16]{1,2,0:T(8,128)} %param.10) | data formatting | bytes 150528 | tf_op args[1]
  2.6 34.6 %moe_input_grad.1 = (bf16[6,196,768]{2,1,0:T(8,128)(2,1)}, f32[1,768]{1,0:T(1,128)}) custom-call(bf16[6,196,768]{2,1,0:T(8,128)(2,1)} %tok_hbm.1, f32[6,196,16]{2,1,0:T(8,128)} %copy.11.log_hbm, bf16[1,96,768]{2,1,0:T(8,128)(2,1)} %so_hbm.1, bf16[1,96,768]{2,1,0:T(8,128)(2,1)} %si_hbm.1, bf16[6,196,768]{2,1,0:T(8,128)(2,1)} %og_hbm.1, ...), custom_call_target="tpu_custom_call" | custom-call | tf_op jit(solution)/shard_map/moe_input_grad/pallas_call | solution.py:209
  37.2 0.0 copy-start
  37.2 2.9 %copy.14 = bf16[6,196,768]{2,1,0:T(8,128)(2,1)} copy(bf16[6,196,768]{2,1,0:T(8,128)(2,1)} %get-tuple-element.4) | data formatting | bytes 3612672
  40.1 0.0 copy-done
  40.1 0.6 %copy.15 = f32[1,768]{1,0:T(1,128)} copy(f32[1,768]{1,0:T(1,128)S(1)} %copy-done) | data formatting | bytes 6144
Async XLA Ops:
  37.2 2.9 %copy-start = (f32[1,768]{1,0:T(1,128)S(1)}, f32[1,768]{1,0:T(1,128)}, u32[]{:S(2)}) copy-start(f32[1,768]{1,0:T(1,128)} %get-tuple-element.5) | copy-start | bytes 9220

commit v2 on v1

--- a/solution.py
+++ b/solution.py
@@ -65,6 +65,10 @@
         loads[name] = pltpu.make_async_copy(src, dst, load_sem.at[at])
         loads[name].start()
 
+    if pad != b:
+        for ref in (recv_s, recv_a, recv_b):
+            ref[...] = jnp.zeros_like(ref)
+
     barrier = pltpu.get_barrier_semaphore()
 
     def greet(d, _):
@@ -76,7 +80,7 @@
 
     def remote(src, dst, send_sem, recv_sem, peer, slot):
         return pltpu.make_async_remote_copy(
-            src_ref=src.at[peer], dst_ref=dst.at[slot], send_sem=send_sem.at[peer],
+            src_ref=src.at[peer, :b], dst_ref=dst.at[slot, :b], send_sem=send_sem.at[peer],
             recv_sem=recv_sem.at[slot], device_id={"exp": peer}, device_id_type=MESH,
         )
 
@@ -113,24 +117,23 @@
     def flat(x):
         return x.astype(F32).reshape(padded, width).astype(BF16)
 
-    loads["so"].wait()
-    send_s[...] = grouped(dot(spread, so[0]))
-    pl.semaphore_wait(barrier, n - 1)
-    send_all(send_s, recv_s, ss, rs)
-
     loads["log"].wait()
     loads["og"].wait()
     for i in range(b):
-        lt = logv[i].T
+        lt = logv[i]
         e = jnp.exp(lt - jnp.max(lt, axis=0, keepdims=True))
         c = e / jnp.sum(e, axis=0, keepdims=True)
         comb[i] = c
         sg[i * n:(i + 1) * n, :] = dot(c.astype(BF16), og[i]).astype(BF16)
     send_a[...] = grouped(dot(to_peers, sg[...]))
+    pl.semaphore_wait(barrier, n - 1)
     send_all(send_a, recv_a, sa, ra)
-
-    for i in range(b):
-        lt = logv[i].T
+    loads["so"].wait()
+    send_s[...] = grouped(dot(spread, so[0]))
+    send_all(send_s, recv_s, ss, rs)
+
+    for i in range(b):
+        lt = logv[i]
         e = jnp.exp(lt - jnp.max(lt, axis=1, keepdims=True))
         disp[i] = e / jnp.sum(e, axis=1, keepdims=True)
 
@@ -202,21 +205,23 @@
     pad = -(-b // 8) * 8
     padded = n * pad
     chunk = 768 if hidden % 768 == 0 else hidden
+    hbm_spec = pl.BlockSpec(memory_space=pltpu.HBM)
     any_spec = pl.BlockSpec(memory_space=pl.ANY)
+    limit = 67043328 - 65536 - b * (-(-seq // 8) * 8) * width * 2
     exchange = pltpu.VMEM((n, pad, width), BF16)
     small = pltpu.VMEM((n, 1, width), F32)
     sems = pltpu.SemaphoreType.DMA((n,))
     return pl.pallas_call(
         functools.partial(body, n, b, pad, chunk),
         out_shape=(
-            jax.ShapeDtypeStruct((b, seq, width), BF16),
-            jax.ShapeDtypeStruct((1, width), F32),
+            pltpu.VMEM((b, seq, width), BF16),
+            pltpu.VMEM((1, width), F32),
         ),
-        in_specs=[any_spec] * 9,
+        in_specs=[hbm_spec] * 9,
         out_specs=(any_spec, pl.BlockSpec(memory_space=pltpu.VMEM)),
         scratch_shapes=[
             pltpu.VMEM(tokens.shape, BF16),
-            pltpu.VMEM(logits.shape, F32),
+            pltpu.VMEM((b, n, seq), F32),
             pltpu.VMEM(slot_out.shape, BF16),
             pltpu.VMEM(slot_in.shape, BF16),
             pltpu.VMEM(out_grad.shape, BF16),
@@ -238,10 +243,10 @@
             sems, sems, sems, sems, sems, sems, sems, sems,
         ],
         compiler_params=pltpu.CompilerParams(
-            collective_id=0, has_side_effects=True, vmem_limit_bytes=60 * 1024 * 1024
+            collective_id=0, has_side_effects=True, vmem_limit_bytes=limit
         ),
         name="moe_input_grad",
-    )(tokens, logits, slot_out, slot_in, out_grad, router, w_in, bias_in, w_out)
+    )(tokens, jnp.swapaxes(logits, 1, 2), slot_out, slot_in, out_grad, router, w_in, bias_in, w_out)
 
 
 def solution(mesh):

time: 40.8 us -> 32 us (0.78)
  Pallas kernels: 34.6 us -> 29.4 us
  local copies, waits for them, and re-layouts: 5.38 us -> 1.81 us
    pallas_call x1, Pallas kernels: 34.6 us -> 29.4 us  [on_device(): pl.pallas_call(functools.partial(body, n, b, pad, chunk), out_shape=(pltp...]
    unnamed x5 -> x2, local copies, waits for them, and re-layouts: 5.38 us -> 1.81 us
where the time goes in v2:
time: 32 us; the launch traced here: 31.9 us
  Pallas kernels  29.4 us (92%)
  local copies, waits for them, and re-layouts  1.81 us (6%)
  between operations  0.64 us (2%)
    pallas_call x1, Pallas kernels, on_device(): pl.pallas_call(functools.partial(body, n, b, pad, chunk), out_shape=(pltp...  29.4 us
    unnamed x2, local copies, waits for them, and re-layouts  1.81 us

profile of v2, /device:TPU:0, one launch (start us, length us, event | category | flops | bytes accessed | tf_op | source)
XLA Modules:
  0.0 31.9 jit_solution(8772994623913234258)
XLA Ops:
  0.6 29.4 %moe_input_grad.1 = (bf16[6,196,768]{2,1,0:T(8,128)(2,1)S(1)}, f32[1,768]{1,0:T(1,128)S(1)}) custom-call(bf16[6,196,768]{2,1,0:T(8,128)(2,1)} %tok_hbm.1, f32[6,16,196]{2,1,0:T(8,128)} %bitcast.1, bf16[1,96,768]{2,1,0:T(8,128)(2,1)} %so_hbm.1, bf16[1,96,768]{2,1,0:T(8,128)(2,1)} %si_hbm.1, bf16[6,196,768]{2,1,0:T(8,128)(2,1)} %og_hbm.1, ...), custom_call_target="tpu_custom_call" | custom-call | tf_op jit(solution)/shard_map/moe_input_grad/pallas_call | solution.py:214
  30.1 1.2 %copy.13 = bf16[6,196,768]{2,1,0:T(8,128)(2,1)} copy(bf16[6,196,768]{2,1,0:T(8,128)(2,1)S(1)} %get-tuple-element.2) | data formatting | bytes 3612672
  31.3 0.6 %copy.14 = f32[1,768]{1,0:T(1,128)} copy(f32[1,768]{1,0:T(1,128)S(1)} %get-tuple-element.3) | data formatting | bytes 6144

commit v3 on v2

--- a/solution.py
+++ b/solution.py
@@ -44,11 +44,11 @@
 def body(
     n, b, pad, chunk,
     tok_hbm, log_hbm, so_hbm, si_hbm, og_hbm, rt_hbm, wi_hbm, bi_hbm, wo_hbm,
-    ig_hbm, rg_ref,
-    tok, logv, so, si, og, rt, wi, bi, wo, igv,
+    ig_ref, rg_ref,
+    tok, logv, so, si, og, rt, wi, bi, wo,
     comb, disp, combl, displ, slope, sg, sip,
-    send_s, recv_s, send_a, recv_a, send_b, recv_b, send_r, recv_r,
-    load_sem, out_sem, ss, rs, sa, ra, sb, rb, sr, rr,
+    send_s, recv_s, send_a, recv_a, send_b, recv_b, send_r, recv_r, tok_t, pre, wi_t,
+    load_sem, sem_a, sem_s, sem_b, sem_r,
 ):
     me = lax.axis_index("exp")
     width = tok.shape[2]
@@ -78,44 +78,45 @@
 
     lax.fori_loop(1, n, greet, 0)
 
-    def remote(src, dst, send_sem, recv_sem, peer, slot):
+    def remote(src, dst, sems, peer):
         return pltpu.make_async_remote_copy(
-            src_ref=src.at[peer, :b], dst_ref=dst.at[slot, :b], send_sem=send_sem.at[peer],
-            recv_sem=recv_sem.at[slot], device_id={"exp": peer}, device_id_type=MESH,
+            src_ref=src.at[peer, :rows_of(src)], dst_ref=dst.at[me, :rows_of(src)], send_sem=sems.at[0],
+            recv_sem=sems.at[1], device_id={"exp": peer}, device_id_type=MESH,
         )
 
-    def send_all(src, dst, send_sem, recv_sem):
-        def step(d, _):
-            remote(src, dst, send_sem, recv_sem, lax.rem(me + d, n), me).start()
+    def rows_of(ref):
+        return min(b, ref.shape[1])
+
+    def send_all(src, dst, sems):
+        def step(k, _):
+            away = n // 2 + (k // 2) * (1 - 2 * (k % 2))
+            remote(src, dst, sems, lax.rem(me + away, n)).start()
             return 0
 
         lax.fori_loop(1, n, step, 0)
         dst[me] = src[me]
 
-    def wait_all(src, dst, send_sem, recv_sem):
-        def step(d, _):
-            peer = lax.rem(me + n - d, n)
-            remote(src, dst, send_sem, recv_sem, peer, peer).wait_recv()
-            return 0
-
-        lax.fori_loop(1, n, step, 0)
-
-    def drain(src, dst, send_sem, recv_sem):
-        def step(d, _):
-            remote(src, dst, send_sem, recv_sem, lax.rem(me + d, n), me).wait_send()
-            return 0
-
-        lax.fori_loop(1, n, step, 0)
+    def everything(src, dst, sems):
+        return pltpu.make_async_remote_copy(
+            src_ref=src.at[:n - 1, :rows_of(src)], dst_ref=dst.at[:n - 1, :rows_of(src)], send_sem=sems.at[0],
+            recv_sem=sems.at[1], device_id={"exp": lax.rem(me + 1, n)}, device_id_type=MESH,
+        )
+
+    def wait_all(src, dst, sems):
+        everything(src, dst, sems).wait_recv()
+
+    def drain(src, dst, sems):
+        everything(src, dst, sems).wait_send()
 
     spread = ones_where(padded, rows, lambda r, c: (r % pad < b) & (c == (r // pad) * b + r % pad))
     to_peers = ones_where(padded, rows, lambda r, c: (r % pad < b) & (c == (r % pad) * n + r // pad))
     to_images = ones_where(rows, padded, lambda r, c: c == (r % n) * pad + r // n)
 
     def grouped(x):
-        return x.reshape(n, pad, width).astype(BF16)
+        return x.reshape(n, pad, x.shape[1]).astype(BF16)
 
     def flat(x):
-        return x.astype(F32).reshape(padded, width).astype(BF16)
+        return x.astype(F32).reshape(padded, x.shape[2]).astype(BF16)
 
     loads["log"].wait()
     loads["og"].wait()
@@ -127,10 +128,10 @@
         sg[i * n:(i + 1) * n, :] = dot(c.astype(BF16), og[i]).astype(BF16)
     send_a[...] = grouped(dot(to_peers, sg[...]))
     pl.semaphore_wait(barrier, n - 1)
-    send_all(send_a, recv_a, sa, ra)
+    send_all(send_a, recv_a, sem_a)
     loads["so"].wait()
     send_s[...] = grouped(dot(spread, so[0]))
-    send_all(send_s, recv_s, ss, rs)
+    send_all(send_s, recv_s, sem_s)
 
     for i in range(b):
         lt = logv[i]
@@ -144,21 +145,23 @@
     for k in range(0, hidden, chunk):
         hp = dot(sip[...], wi[0, :, k:k + chunk]) + bi[:, k:k + chunk]
         slope[:, k:k + chunk] = gelu_slope(hp)
+        wi_t[k:k + chunk, :] = wi[0, :, k:k + chunk].T
 
     loads["wo"].wait()
-    wait_all(send_a, recv_a, sa, ra)
+    wait_all(send_a, recv_a, sem_a)
     got = flat(recv_a[...])
-    acc = jnp.zeros((padded, width), F32)
     for k in range(0, hidden, chunk):
         hg = dot_nt(got, wo[0, k:k + chunk, :])
-        pre = (hg * slope[:, k:k + chunk]).astype(BF16)
-        acc = acc + dot_nt(pre, wi[0, :, k:k + chunk])
-    send_b[...] = grouped(acc)
-    send_all(send_b, recv_b, sb, rb)
+        pre[:, k:k + chunk] = (hg * slope[:, k:k + chunk]).astype(BF16)
+    blocks, block = send_b.shape[0], send_b.shape[3]
+    for q in range(blocks):
+        acc = dot(pre[...], wi_t[:, q * block:(q + 1) * block])
+        send_b[q] = grouped(acc)
+        send_all(send_b.at[q], recv_b.at[q], sem_b.at[q])
 
     loads["tok"].wait()
     loads["rt"].wait()
-    wait_all(send_s, recv_s, ss, rs)
+    wait_all(send_s, recv_s, sem_s)
     outs = dot(to_images, flat(recv_s[...])).astype(BF16)
     racc = jnp.zeros((n, width), F32)
     for i in range(b):
@@ -167,35 +170,32 @@
         cl = (c * (cg - jnp.sum(c * cg, axis=0, keepdims=True))).astype(BF16)
         combl[i] = cl
         racc = racc + dot(cl, tok[i])
-
-    wait_all(send_b, recv_b, sb, rb)
-    sg[...] = dot(to_images, flat(recv_b[...])).astype(BF16)
-    for i in range(b):
-        dg = dot_nt(sg[i * n:(i + 1) * n, :], tok[i])
+        tok_t[i] = tok[i].T
+
+    for q in range(blocks):
+        wait_all(send_b.at[q], recv_b.at[q], sem_b.at[q])
+        sg[:, q * block:(q + 1) * block] = dot(to_images, flat(recv_b[q])).astype(BF16)
+    for i in range(b):
+        dg = dot(sg[i * n:(i + 1) * n, :], tok_t[i])
         d = disp[i]
         dl = (d * (dg - jnp.sum(d * dg, axis=1, keepdims=True))).astype(BF16)
         displ[i] = dl
         racc = racc + dot(dl, tok[i])
     send_r[...] = racc.reshape(n, 1, width)
-    send_all(send_r, recv_r, sr, rr)
-
-    outs_dma = []
+    send_all(send_r, recv_r, sem_r)
+
     for i in range(b):
         left = jnp.concatenate([disp[i].astype(BF16), combl[i], displ[i]], axis=0)
         right = jnp.concatenate([sg[i * n:(i + 1) * n, :], rt[...], rt[...]], axis=0)
-        igv[i] = dot_tn(left, right).astype(BF16)
-        copy = pltpu.make_async_copy(igv.at[i], ig_hbm.at[i], out_sem.at[i])
-        copy.start()
-        outs_dma.append(copy)
-
-    wait_all(send_r, recv_r, sr, rr)
+        ig_ref[i] = dot_tn(left, right).astype(BF16)
+
+    drain(send_s, recv_s, sem_s)
+    drain(send_a, recv_a, sem_a)
+    for q in range(blocks):
+        drain(send_b.at[q], recv_b.at[q], sem_b.at[q])
+    wait_all(send_r, recv_r, sem_r)
     rg_ref[...] = jnp.sum(recv_r[...], axis=0) / (n * b)
-    drain(send_s, recv_s, ss, rs)
-    drain(send_a, recv_a, sa, ra)
-    drain(send_b, recv_b, sb, rb)
-    drain(send_r, recv_r, sr, rr)
-    for copy in outs_dma:
-        copy.wait()
+    drain(send_r, recv_r, sem_r)
 
 
 def on_device(tokens, logits, slot_out, slot_in, out_grad, router, w_in, bias_in, w_out):
@@ -206,11 +206,12 @@
     padded = n * pad
     chunk = 768 if hidden % 768 == 0 else hidden
     hbm_spec = pl.BlockSpec(memory_space=pltpu.HBM)
-    any_spec = pl.BlockSpec(memory_space=pl.ANY)
     limit = 67043328 - 65536 - b * (-(-seq // 8) * 8) * width * 2
     exchange = pltpu.VMEM((n, pad, width), BF16)
     small = pltpu.VMEM((n, 1, width), F32)
-    sems = pltpu.SemaphoreType.DMA((n,))
+    sems = pltpu.SemaphoreType.DMA((2,))
+    block = 256 if width % 256 == 0 else width
+    columns = pltpu.VMEM((width // block, n, pad, block), BF16)
     return pl.pallas_call(
         functools.partial(body, n, b, pad, chunk),
         out_shape=(
@@ -218,7 +219,7 @@
             pltpu.VMEM((1, width), F32),
         ),
         in_specs=[hbm_spec] * 9,
-        out_specs=(any_spec, pl.BlockSpec(memory_space=pltpu.VMEM)),
+        out_specs=(pl.BlockSpec(memory_space=pltpu.VMEM), pl.BlockSpec(memory_space=pltpu.VMEM)),
         scratch_shapes=[
             pltpu.VMEM(tokens.shape, BF16),
             pltpu.VMEM((b, n, seq), F32),
@@ -229,7 +230,6 @@
             pltpu.VMEM(w_in.shape, BF16),
             pltpu.VMEM(bias_in.shape, F32),
             pltpu.VMEM(w_out.shape, BF16),
-            pltpu.VMEM((b, seq, width), BF16),
             pltpu.VMEM((b, n, seq), F32),
             pltpu.VMEM((b, n, seq), F32),
             pltpu.VMEM((b, n, seq), BF16),
@@ -237,10 +237,12 @@
             pltpu.VMEM((padded, hidden), F32),
             pltpu.VMEM((n * b, width), BF16),
             pltpu.VMEM((padded, width), BF16),
-            exchange, exchange, exchange, exchange, exchange, exchange, small, small,
+            exchange, exchange, exchange, exchange, columns, columns, small, small,
+            pltpu.VMEM((b, width, seq), BF16),
+            pltpu.VMEM((padded, hidden), BF16),
+            pltpu.VMEM((hidden, width), BF16),
             pltpu.SemaphoreType.DMA((9,)),
-            pltpu.SemaphoreType.DMA((b,)),
-            sems, sems, sems, sems, sems, sems, sems, sems,
+            sems, sems, pltpu.SemaphoreType.DMA((width // block, 2)), sems,
         ],
         compiler_params=pltpu.CompilerParams(
             collective_id=0, has_side_effects=True, vmem_limit_bytes=limit

time: 32 us -> 29.2 us (0.912)
  Pallas kernels: 29.4 us -> 26.6 us
    pallas_call x1, Pallas kernels: 29.4 us -> 26.6 us  [on_device(): pl.pallas_call(functools.partial(body, n, b, pad, chunk), out_shape=(pltp...]
where the time goes in v3:
time: 29.2 us; the launch traced here: 29 us
  Pallas kernels  26.6 us (91%)
  local copies, waits for them, and re-layouts  1.81 us (6%)
  between operations  0.64 us (2%)
    pallas_call x1, Pallas kernels, on_device(): pl.pallas_call(functools.partial(body, n, b, pad, chunk), out_shape=(pltp...  26.6 us
    unnamed x2, local copies, waits for them, and re-layouts  1.81 us

profile of v3, /device:TPU:0, one launch (start us, length us, event | category | flops | bytes accessed | tf_op | source)
XLA Modules:
  0.0 29.0 jit_solution(3567605878414615365)
XLA Ops:
  0.6 26.6 %moe_input_grad.1 = (bf16[6,196,768]{2,1,0:T(8,128)(2,1)S(1)}, f32[1,768]{1,0:T(1,128)S(1)}) custom-call(bf16[6,196,768]{2,1,0:T(8,128)(2,1)} %tok_hbm.1, f32[6,16,196]{2,1,0:T(8,128)} %bitcast.1, bf16[1,96,768]{2,1,0:T(8,128)(2,1)} %so_hbm.1, bf16[1,96,768]{2,1,0:T(8,128)(2,1)} %si_hbm.1, bf16[6,196,768]{2,1,0:T(8,128)(2,1)} %og_hbm.1, ...), custom_call_target="tpu_custom_call" | custom-call | tf_op jit(solution)/shard_map/moe_input_grad/pallas_call | solution.py:215
  27.2 1.2 %copy.13 = bf16[6,196,768]{2,1,0:T(8,128)(2,1)} copy(bf16[6,196,768]{2,1,0:T(8,128)(2,1)S(1)} %get-tuple-element.2) | data formatting | bytes 3612672
  28.5 0.6 %copy.14 = f32[1,768]{1,0:T(1,128)} copy(f32[1,768]{1,0:T(1,128)S(1)} %get-tuple-element.3) | data formatting | bytes 6144

commit v4 on v3

--- a/solution.py
+++ b/solution.py
@@ -76,7 +76,7 @@
         pl.semaphore_signal(barrier, inc=1, device_id={"exp": peer}, device_id_type=MESH)
         return 0
 
-    lax.fori_loop(1, n, greet, 0)
+    lax.fori_loop(1, n, greet, 0, unroll=True)
 
     def remote(src, dst, sems, peer):
         return pltpu.make_async_remote_copy(
@@ -93,7 +93,7 @@
             remote(src, dst, sems, lax.rem(me + away, n)).start()
             return 0
 
-        lax.fori_loop(1, n, step, 0)
+        lax.fori_loop(1, n, step, 0, unroll=True)
         dst[me] = src[me]
 
     def everything(src, dst, sems):
@@ -210,7 +210,7 @@
     exchange = pltpu.VMEM((n, pad, width), BF16)
     small = pltpu.VMEM((n, 1, width), F32)
     sems = pltpu.SemaphoreType.DMA((2,))
-    block = 256 if width % 256 == 0 else width
+    block = width // 2 if width % 256 == 0 else width
     columns = pltpu.VMEM((width // block, n, pad, block), BF16)
     return pl.pallas_call(
         functools.partial(body, n, b, pad, chunk),

time: 29.2 us -> 28.5 us (0.976)
  Pallas kernels: 26.6 us -> 25.9 us
    pallas_call x1, Pallas kernels: 26.6 us -> 25.9 us  [on_device(): pl.pallas_call(functools.partial(body, n, b, pad, chunk), out_shape=(pltp...]
where the time goes in v4:
time: 28.5 us; the launch traced here: 28.4 us
  Pallas kernels  25.9 us (91%)
  local copies, waits for them, and re-layouts  1.81 us (6%)
  between operations  0.64 us (2%)
    pallas_call x1, Pallas kernels, on_device(): pl.pallas_call(functools.partial(body, n, b, pad, chunk), out_shape=(pltp...  25.9 us
    unnamed x2, local copies, waits for them, and re-layouts  1.81 us

profile of v4, /device:TPU:0, one launch (start us, length us, event | category | flops | bytes accessed | tf_op | source)
XLA Modules:
  0.0 28.4 jit_solution(16907320997111294046)
XLA Ops:
  0.6 25.9 %moe_input_grad.1 = (bf16[6,196,768]{2,1,0:T(8,128)(2,1)S(1)}, f32[1,768]{1,0:T(1,128)S(1)}) custom-call(bf16[6,196,768]{2,1,0:T(8,128)(2,1)} %tok_hbm.1, f32[6,16,196]{2,1,0:T(8,128)} %bitcast.1, bf16[1,96,768]{2,1,0:T(8,128)(2,1)} %so_hbm.1, bf16[1,96,768]{2,1,0:T(8,128)(2,1)} %si_hbm.1, bf16[6,196,768]{2,1,0:T(8,128)(2,1)} %og_hbm.1, ...), custom_call_target="tpu_custom_call" | custom-call | tf_op jit(solution)/shard_map/moe_input_grad/pallas_call | solution.py:215
  26.6 1.2 %copy.13 = bf16[6,196,768]{2,1,0:T(8,128)(2,1)} copy(bf16[6,196,768]{2,1,0:T(8,128)(2,1)S(1)} %get-tuple-element.2) | data formatting | bytes 3612672
  27.8 0.6 %copy.14 = f32[1,768]{1,0:T(1,128)} copy(f32[1,768]{1,0:T(1,128)S(1)} %get-tuple-element.3) | data formatting | bytes 6144
